TPU v7x, 32 devices: a whole 2x2x4 slice. The times are simulated.
32 devices in a mesh: seq: 4 (over z), tp: 4 (over y, x), dp: 2 (over core).
Axes of the slice: x: 2, y: 2, z: 4, core: 2. Of those that a mesh axis runs over, the one named last changes fastest.
Arguments:
- x_ckpt: bfloat16 [1024, 5120], P(('dp', 'seq', 'tp')), parts along dimension 0, may hold values from -5 to 5
- bc_ckpt: bfloat16 [2, 1024, 128], P(None, ('dp', 'seq', 'tp')), parts along dimension 1, may hold values from -1 to 1
- step_sizes: float32 [80, 1024], P('tp', ('dp', 'seq')), parts along dimension 1, may hold values from 0.03 to 0.3
- decay_rate: float32 [80], P('tp'), may hold values from 0 to 1, as said below
- skip_gain: float32 [80], P('tp'), may hold values from 0.25 to 1.75
- grad_out: bfloat16 [1024, 5120], P(('dp', 'seq'), 'tp'), parts along dimension 0, may hold values from -3 to 3
Outputs:
- grad_x: bfloat16 [1024, 5120], P(('dp', 'seq'), 'tp'), parts along dimension 0
- grad_bc: float32 [2, 1024, 128], P(None, ('dp', 'seq', 'tp')), parts along dimension 1
- grad_step: float32 [80, 1024], P('tp', ('dp', 'seq')), parts along dimension 1
There are 2 independent parts, one for each index of `dp`. A program takes and returns all parts, laid end to end along the dimension named above; an argument that names none is the same for every part. Nothing has to cross between parts.
Inputs may be any that keep to these rules, and one draw needn't show every extreme that they name: `decay_rate`: positive decay rates of the 80 heads.
All inputs are finite; a program needn't handle non-finite values.
Results may differ from a plain program's by a relative error of at most 0.001.
Values may be sent and summed in bfloat16 or wider, within the bound.
A program may use at most 128 MiB of HBM per device.

v0:
```python
from functools import partial

import jax
import jax.numpy as jnp
from jax import lax
from jax.sharding import PartitionSpec as P

BLOCK = 128


highest = lax.Precision.HIGHEST


def carried_in(array, axis, combine, identity, reverse):
    peers, index = (lax.axis_size(axis), lax.axis_index(axis))
    everything = jax.tree.map(lambda part: lax.all_gather(part, axis), array)
    start = jax.tree.map(
        lambda part, zero: jnp.broadcast_to(jnp.asarray(zero, part.dtype), part.shape),
        array,
        identity,
    )

    def hop(k, before):
        at = peers - 1 - k if reverse else k
        reached = at > index if reverse else at < index
        new = combine(before, jax.tree.map(lambda part: part[at], everything))
        return jax.tree.map(lambda a, b: jnp.where(reached, a, b), new, before)

    return lax.fori_loop(0, peers, hop, start)


def block_step(head_rates, head_gains, carry_state, pieces):
    inputs, step_block, proj_b, proj_c = pieces
    head_count = step_block.shape[0]
    row_count = step_block.shape[1]
    values = inputs.astype(jnp.float32).reshape(row_count, head_count, -1)
    cumulative = jnp.cumsum(-head_rates[:, None] * step_block, axis=1)
    positions = jnp.arange(row_count, dtype=jnp.int32)
    causal = positions[:, None] >= positions[None, :]
    log_gaps = cumulative[:, :, None] - cumulative[:, None, :]
    within = jnp.where(causal, jnp.exp(jnp.where(causal, log_gaps, 0.0)), 0.0)
    scores = jnp.dot(proj_c, proj_b.T, precision=highest, preferred_element_type=jnp.float32)
    weights = within * scores[None, :, :] * step_block[:, None, :]
    local_part = jnp.einsum(
        "hts,shp->thp", weights, values, precision=highest, preferred_element_type=jnp.float32
    )
    carried = jnp.einsum(
        "tn,hpn->thp", proj_c, carry_state, precision=highest, preferred_element_type=jnp.float32
    )
    carried = carried * jnp.exp(cumulative).T[:, :, None]
    result = local_part + carried + head_gains[None, :, None] * values
    tail_weight = jnp.exp(cumulative[:, -1:] - cumulative) * step_block
    fresh_state = jnp.einsum(
        "hs,shp,sn->hpn",
        tail_weight,
        values,
        proj_b,
        precision=highest,
        preferred_element_type=jnp.float32,
    )
    final_state = jnp.exp(cumulative[:, -1])[:, None, None] * carry_state + fresh_state
    return (final_state, result.reshape(row_count, -1))


def run_blocks(inputs, step_sizes, proj_b, proj_c, start_state, head_rates, head_gains, block_rows):
    row_count = inputs.shape[0]
    block_count = row_count // block_rows
    head_count = step_sizes.shape[0]
    input_blocks = inputs.reshape(block_count, block_rows, inputs.shape[1])
    step_blocks = step_sizes.reshape(head_count, block_count, block_rows).transpose(1, 0, 2)
    b_blocks = proj_b.reshape(block_count, block_rows, proj_b.shape[1])
    c_blocks = proj_c.reshape(block_count, block_rows, proj_c.shape[1])
    stepper = jax.checkpoint(partial(block_step, head_rates, head_gains))
    final_state, results = lax.scan(
        stepper, start_state, (input_blocks, step_blocks, b_blocks, c_blocks)
    )
    return (results.reshape(row_count, -1), final_state)


def combine(earlier, later):
    return (earlier[0] * later[0], later[0][:, None, None] * earlier[1] + later[1])


def shards(x_ckpt, bc_ckpt, step_sizes, decay_rate, skip_gain, grad_out):
    head_count = decay_rate.shape[0]
    width = grad_out.shape[1]
    own_rows = lax.all_to_all(x_ckpt, "tp", split_axis=1, concat_axis=0, tiled=True)
    pairs = lax.all_gather(bc_ckpt, "tp", axis=1, tiled=True)
    proj_b = pairs[0].astype(jnp.float32)
    proj_c = pairs[1].astype(jnp.float32)
    token_count = own_rows.shape[0]
    head_width = width // head_count
    values = own_rows.astype(jnp.float32).reshape(token_count, head_count, head_width)
    cumulative = jnp.cumsum(-decay_rate[:, None] * step_sizes, axis=1)
    passing = jnp.exp(cumulative[:, -1])
    tail_weight = jnp.exp(cumulative[:, -1:] - cumulative) * step_sizes
    summary = jnp.einsum(
        "hs,shp,sn->hpn",
        tail_weight,
        values,
        proj_b,
        precision=highest,
        preferred_element_type=jnp.float32,
    )
    upstream = grad_out.astype(jnp.float32)
    pulled = jnp.einsum(
        "ht,thp,tn->hpn",
        jnp.exp(cumulative),
        upstream.reshape(token_count, head_count, head_width),
        proj_c,
        precision=highest,
        preferred_element_type=jnp.float32,
    )
    neutral = (jnp.ones_like(passing), jnp.zeros_like(summary))
    entering = carried_in((passing, summary), "seq", combine, neutral, False)[1]
    leaving = carried_in((passing, pulled), "seq", combine, neutral, True)[1]

    def forward(inputs, basis_b, basis_c, step_block, start_state):
        return run_blocks(
            inputs, step_block, basis_b, basis_c, start_state, decay_rate, skip_gain, BLOCK
        )

    outputs, pull_back = jax.vjp(forward, own_rows, proj_b, proj_c, step_sizes, entering)
    grad_x, grad_b, grad_c, grad_step, unused = pull_back((upstream, leaving))
    partial_grads = jnp.stack([grad_b, grad_c])
    grad_bc = lax.psum_scatter(partial_grads, "tp", scatter_dimension=1, tiled=True)
    return (grad_x, grad_bc, grad_step)


def solution(mesh):
    return jax.shard_map(
        shards,
        mesh=mesh,
        in_specs=(
            P(("dp", "seq", "tp"), None),
            P(None, ("dp", "seq", "tp"), None),
            P("tp", ("dp", "seq")),
            P("tp"),
            P("tp"),
            P(("dp", "seq"), "tp"),
        ),
        out_specs=(
            P(("dp", "seq"), "tp"),
            P(None, ("dp", "seq", "tp"), None),
            P("tp", ("dp", "seq")),
        ),
        check_vma=False,
    )
```

profile of v0, /device:TPU:0, one launch (start us, length us, event | category | flops | bytes accessed | tf_op | source)
XLA Modules:
  0.0 178.6 jit_solution(7967003669195045583)
XLA Ops:
  7.9 0.8 broadcast_multiply_fusion.2
  9.1 0.8 exponential_bitcast_fusion
  9.9 9.9 %all_gather.22 = bf16[2,128,128]{2,1,0:T(8,128)(2,1)S(1)} all-gather(bf16[2,32,128]{2,1,0:T(8,128)(2,1)} %param.11), channel_id=1, replica_groups=mesh['seq'=4,'tp'=4,'dp'=2] {'tp'}, dimensions={1}, use_global_device_ids=true | all-gather | bytes 81920 | tf_op jit(solution)/shard_map/all_gather | solution.py:88
  19.8 1.2 copy.35
  21.1 1.3 fusion.32
  22.4 0.7 copy.53
  23.1 3.5 %all-to-all-start = ((bf16[32,4,1280]{2,0,1:T(8,128)(2,1)}), bf16[32,4,1280]{2,0,1:T(8,128)(2,1)S(1)}, u32[]{:S(2)}, u32[]{:S(2)}) async-start(bf16[32,4,1280]{2,0,1:T(8,128)(2,1)} %bitcast.97), calls=%async_computation | async-start | bytes 655360 | tf_op jit(solution)/shard_map/all_to_all | solution.py:87
  26.7 5.4 %all-to-all-done = bf16[32,4,1280]{2,0,1:T(8,128)(2,1)S(1)} async-done(((bf16[32,4,1280]{2,0,1:T(8,128)(2,1)}), bf16[32,4,1280]{2,0,1:T(8,128)(2,1)S(1)}, u32[]{:S(2)}, u32[]{:S(2)}) %all-to-all-start) | async-done | bytes 327712 | tf_op jit(solution)/shard_map/all_to_all | solution.py:87
  33.3 2.0 %fusion.2 = f32[20,64,128]{2,1,0:T(8,128)} fusion(f32[128,20,64]{2,1,0:T(8,128)S(1)} %broadcast_multiply_fusion, bf16[2,128,128]{2,1,0:T(8,128)(2,1)S(1)} %all_gather.22), kind=kOutput, calls=%fused_computation.6 | convolution fusion | flops 251658240 | bytes 2260992 | tf_op jit(solution)/shard_map/hs,shp,sn->hpn/dot_general | solution.py:97
  37.0 12.7 %all-reduce.2 = f32[80]{0:T(128)S(1)} all-reduce(f32[80]{0:T(128)S(1)} %dynamic-update-slice), channel_id=2, replica_groups=mesh['seq'=4,'tp'=4,'dp'=2] {'seq'}, use_global_device_ids=true, to_apply=%add.2 | all-reduce | flops 80 | bytes 640
  49.8 0.8 bitcast_convert_fusion.1
  50.6 27.2 %all-gather.8.cloned.1.call-done = f32[80,64,128]{2,1,0:T(8,128)} async-done(((f32[20,64,128]{2,1,0:T(8,128)}), f32[80,64,128]{2,1,0:T(8,128)}) %all-gather.8.cloned.1.call-update) | async-done | bytes 2621456 | tf_op jit(solution)/shard_map/all_gather | solution.py:16
  77.7 5.1 %while.21 = (s32[]{:T(128)}, f32[20,64,128]{2,1,0:T(8,128)S(1)}, s32[]{:T(128)}, f32[4,20]{1,0:T(4,128)S(1)}, f32[4,20,64,128]{3,2,1,0:T(8,128)}, /*index=5*/s32[]{:T(128)}, s32[]{:T(128)}, s32[]{:T(128)}, s32[]{:T(128)}) while((s32[]{:T(128)}, f32[20,64,128]{2,1,0:T(8,128)S(1)}, s32[]{:T(128)}, f32[4,20]{1,0:T(4,128)S(1)}, ...), condition=%wide.region_4.5_spmd.clone, body=%wide.region_3.4_spmd.clone.sunk | while | flops 655368 | bytes 1966487 | solution.py:29
  77.8 1.2 fusion.67
  79.0 1.2 fusion.67
  80.3 1.2 fusion.67
  81.6 1.2 fusion.67
  82.8 50.0 %all-gather.6.cloned.1.call-done = f32[80,64,128]{2,1,0:T(8,128)} async-done(((f32[20,64,128]{2,1,0:T(8,128)}), f32[80,64,128]{2,1,0:T(8,128)}) %all-gather.6.cloned.1.call-update) | async-done | bytes 2621456 | tf_op jit(solution)/shard_map/all_gather | solution.py:16
  132.8 5.1 %while.20 = (s32[]{:T(128)}, f32[20,64,128]{2,1,0:T(8,128)S(1)}, s32[]{:T(128)}, f32[4,20]{1,0:T(4,128)S(1)}, f32[4,20,64,128]{3,2,1,0:T(8,128)}, /*index=5*/s32[]{:T(128)}, s32[]{:T(128)}) while((s32[]{:T(128)}, f32[20,64,128]{2,1,0:T(8,128)S(1)}, s32[]{:T(128)}, f32[4,20]{1,0:T(4,128)S(1)}, f32[4,20,64,128]{3,2,1,0:T(8,128)}, ...), condition=%wide.region_2.3_spmd.clone, body=%wide.region_1.2_spmd.clone.sunk | while | flops 655364 | bytes 1966425 | solution.py:29
  132.8 1.2 fusion.66
  134.1 1.2 fusion.66
  135.4 1.2 fusion.66
  136.7 1.2 fusion.66
  139.3 0.7 fusion.23
  140.5 0.7 fusion.18
  141.2 2.2 %fusion.22 = (f32[20,128]{1,0:T(8,128)S(1)}, f32[20,128]{1,0:T(8,128)S(1)}, f32[20,128]{1,0:T(8,128)S(1)}, f32[128,128]{1,0:T(8,128)S(1)}) fusion(f32[20,128]{1,0:T(8,128)S(1)} %copy-done.4, f32[128,128]{1,0:T(8,128)S(1)} %fusion.50, f32[20,128]{1,0:T(8,128)S(1)} %reduce_window_sum.35, pred[128,128]{1,0:T(8,128)(4,1)S(1)} %iota_compare_fusion, ...), kind=kOutput, calls=%fused_computation.29 | convolution fusion | flops 256549376 | bytes 1181696 | tf_op jit(solution)/shard_map/transpose(jvp())/while/body/eval_jaxpr/checkpoint/hts,shp->thp/dot_general | solution.py:44
  143.5 1.2 convolution_bitcast_fusion.1
  144.7 1.2 reduce_window_sum.36
  146.6 1.2 convolution_bitcast_fusion
  149.0 1.6 fusion.15
  150.7 0.9 copy.39
  151.6 20.5 %reduce-scatter.2.cloned.1.call-done = f32[2,32,128]{2,1,0:T(8,128)} async-done(((f32[2,128,128]{2,1,0:T(8,128)}), f32[2,32,128]{2,1,0:T(8,128)}) %reduce-scatter.2.cloned.1.call-update) | async-done | bytes 32784 | tf_op jit(solution)/shard_map/reduce_scatter | solution.py:126
  (60 shorter events, 7.4 us)
Async XLA Ops:
  7.2 70.6 %all-gather.8.cloned.1.call-start = ((), (), s32[]{:S(2)}) async-start(), calls=%async_computation.4 | async-start | bytes 3276800 | tf_op jit(solution)/shard_map/all_gather | solution.py:16
  19.8 13.5 %copy-start.2 = (bf16[2,128,128]{2,1,0:T(8,128)(2,1)}, bf16[2,128,128]{2,1,0:T(8,128)(2,1)S(1)}, u32[]{:S(2)}) copy-start(bf16[2,128,128]{2,1,0:T(8,128)(2,1)S(1)} %all_gather.22) | copy-start | bytes 196612
  21.0 1.4 copy-start.3
  23.1 9.0 %all-to-all-start = ((bf16[32,4,1280]{2,0,1:T(8,128)(2,1)}), bf16[32,4,1280]{2,0,1:T(8,128)(2,1)S(1)}, u32[]{:S(2)}, u32[]{:S(2)}) async-start(bf16[32,4,1280]{2,0,1:T(8,128)(2,1)} %bitcast.97), calls=%async_computation | async-start | bytes 655360 | tf_op jit(solution)/shard_map/all_to_all | solution.py:87
  26.6 106.2 %all-gather.6.cloned.1.call-start = ((), (), s32[]{:S(2)}) async-start(), calls=%async_computation.3 | async-start | bytes 3276800 | tf_op jit(solution)/shard_map/all_gather | solution.py:16
  32.1 0.7 copy-start
  33.3 2.2 %copy-start.7 = (u32[32]{0:T(128)S(1)}, u32[32]{0:T(128)}, u32[]{:S(2)}) copy-start(u32[32]{0:T(128)} %constant.131) | copy-start | bytes 388
  35.4 136.7 %reduce-scatter.2.cloned.1.call-start = ((), (), s32[]{:S(2)}) async-start(), calls=%async_computation.2 | async-start | bytes 163840 | tf_op jit(solution)/shard_map/reduce_scatter | solution.py:126
  132.8 5.1 %copy-start.5 = (f32[20]{0:T(128)S(1)}, f32[20]{0:T(128)}, u32[]{:S(2)}) copy-start(f32[20]{0:T(128)} %param.13) | copy-start | bytes 244
  132.8 5.1 %copy-start.4 = (f32[20,128]{1,0:T(8,128)S(1)}, f32[20,128]{1,0:T(8,128)}, u32[]{:S(2)}) copy-start(f32[20,128]{1,0:T(8,128)} %param.12) | copy-start | bytes 30724
  137.9 1.0 copy-start.1
  144.7 4.3 %copy-start.6 = (f32[20]{0:T(128)S(1)}, f32[20]{0:T(128)}, u32[]{:S(2)}) copy-start(f32[20]{0:T(128)} %param.14) | copy-start | bytes 244
Sparse Core Ops, SparseCore 0:
  22.5 55.2 all-gather.7
  79.3 53.4 all-gather.5
  149.2 22.8 reduce-scatter.1
where the time goes:
time: 179 us
  waiting for transfers between devices  103 us (58%)
  blocking collectives  22.6 us (13%)
  other arithmetic  17.4 us (10%)
  between operations  14.6 us (8%)
  matrix products  11.7 us (7%)
  local copies, waits for them, and re-layouts  5.46 us (3%)
  starting transfers between devices  3.58 us (2%)
    all_gather x2, waiting for transfers between devices, carried_in(): everything = jax.tree.map(lambda part: lax.all_gather(part, axis), array)  77.2 us
    reduce_scatter x1, waiting for transfers between devices, shards(): lax.psum_scatter(partial_grads, 'tp', scatter_dimension=1, tiled=True)  20.5 us
    unnamed x1, blocking collectives  12.7 us
    all_gather x1, blocking collectives, shards(): pairs = lax.all_gather(bc_ckpt, 'tp', axis=1, tiled=True)  9.88 us
    select_n x8, other arithmetic, hop(): return jax.tree.map(lambda a, b: jnp.where(reached, a, b), new, before)  9.87 us
    all_to_all x1, waiting for transfers between devices, shards(): lax.all_to_all(x_ckpt, 'tp', split_axis=1, concat_axis=0, tiled=True)  5.35 us
    dot_general x2, matrix products, block_step(): jnp.einsum('hts,shp->thp', weights, values, precision=highest, preferred_...  3.77 us
  transfers between devices with their start and end apart: 4, of which 4 were waited for; matrix products, arithmetic and copies ran while one was open for 7% of the time, Pallas kernels for 0%

commit v1 on v0

v1 whole, which is shorter than its diff:
```python
from functools import partial

import jax
import jax.numpy as jnp
from jax import lax
from jax.experimental import pallas as pl
from jax.experimental.pallas import tpu as pltpu
from jax.sharding import PartitionSpec as P

MESH = pl.DeviceIdType.MESH
F32 = jnp.float32
BF16 = jnp.bfloat16
HEAD_PAD = 32
SKEW = 2

NN = (((1,), (0,)), ((), ()))
NT = (((1,), (1,)), ((), ()))


def dot(a, b, dims=NN):
    return lax.dot_general(a, b, dims, preferred_element_type=F32)


def exact(a, b):
    return lax.dot_general(
        a, b, NN, precision=lax.Precision.HIGHEST, preferred_element_type=F32
    )


def split(v):
    high = v.astype(BF16)
    return high, (v - high.astype(F32)).astype(BF16)


def dot2(a, b, dims=NN):
    return dot(a, b[0], dims) + dot(a, b[1], dims)


def dot2l(a, b, dims=NN):
    return dot(a[0], b, dims) + dot(a[1], b, dims)


def dot3(a, b, dims=NN):
    return dot(a[0], b[0], dims) + (dot(a[0], b[1], dims) + dot(a[1], b[0], dims))


def kernel(
    peers, blocks, head_width,
    x_ref, bc_ref, step_ref, rate_ref, gain_ref, dy_ref,
    gx_ref, gbc_ref, gstep_ref,
    xr, bcr, part, rs,
    state_in, state_out, pull_in, pull_out, fresh, pulled, a2_loc, z_loc,
    xs_h, xs_l, ys_h, ys_l, xc, dyc, ec, ed, gain_row,
    stp, rates, gains, cums, mt_acc, bc_acc, dcum_acc, dir_acc, sm, bcm,
    send_x, recv_x, send_b, recv_b, own_sem,
    send_f, recv_f, send_g, recv_g, send_r, recv_r,
):
    me = lax.axis_index("tp")
    block = lax.axis_index("seq")
    head_count, tokens = step_ref.shape
    width = dy_ref.shape[1]
    rows = x_ref.shape[0]
    chunks, _, lanes = xc.shape
    chunk_heads = lanes // head_width

    has_prev = block > 0
    has_next = block < blocks - 1

    barrier = pltpu.get_barrier_semaphore()
    for d in range(1, peers):
        pl.semaphore_signal(
            barrier, inc=1, device_id={"tp": lax.rem(me + d, peers)}, device_id_type=MESH
        )

    @pl.when(has_prev)
    def _():
        pl.semaphore_signal(barrier, inc=1, device_id={"seq": block - 1}, device_id_type=MESH)

    @pl.when(has_next)
    def _():
        pl.semaphore_signal(barrier, inc=1, device_id={"seq": block + 1}, device_id_type=MESH)

    neighbours = jnp.where(has_prev, 1, 0) + jnp.where(has_next, 1, 0)
    pl.semaphore_wait(barrier, peers - 1 + neighbours)

    def bc_copy(peer, slot):
        return pltpu.make_async_remote_copy(
            src_ref=bc_ref, dst_ref=bcr.at[slot],
            send_sem=send_b.at[peer], recv_sem=recv_b.at[slot],
            device_id={"tp": peer}, device_id_type=MESH,
        )

    def x_copy(peer, slot):
        return pltpu.make_async_remote_copy(
            src_ref=x_ref.at[:, pl.ds(pl.multiple_of(peer * width, 128), width)],
            dst_ref=xr.at[slot],
            send_sem=send_x.at[peer], recv_sem=recv_x.at[slot],
            device_id={"tp": peer}, device_id_type=MESH,
        )

    for d in range(1, peers):
        bc_copy(lax.rem(me + d, peers), me).start()
    for d in range(1, peers):
        x_copy(lax.rem(me + d, peers), me).start()
    own_x = pltpu.make_async_copy(
        x_ref.at[:, pl.ds(pl.multiple_of(me * width, 128), width)], xr.at[me], own_sem.at[0]
    )
    own_bc = pltpu.make_async_copy(bc_ref, bcr.at[me], own_sem.at[1])
    own_x.start()
    own_bc.start()

    stp[...] = jnp.zeros_like(stp)
    stp[0:head_count] = step_ref[...]
    rates[...] = jnp.zeros_like(rates)
    gains[...] = jnp.zeros_like(gains)
    for h in range(head_count):
        rates[h : h + 1] = jnp.full((1, tokens), rate_ref[h], F32)
        gains[h : h + 1] = jnp.full((1, tokens), gain_ref[h], F32)
    row = lax.broadcasted_iota(jnp.int32, (tokens, tokens), 0)
    col = lax.broadcasted_iota(jnp.int32, (tokens, tokens), 1)
    upto = row <= col
    cum = exact(-rates[...] * stp[...], jnp.where(upto, 1.0, 0.0).astype(F32))
    cums[...] = cum
    stacked = jnp.concatenate(
        [jnp.exp(cum), jnp.exp(-cum) * stp[...], gains[...], jnp.zeros_like(cum)], axis=0
    )
    table = split(stacked.T)
    pick_row = lax.broadcasted_iota(jnp.int32, (4 * HEAD_PAD, lanes), 0)
    pick_head = lax.broadcasted_iota(jnp.int32, (4 * HEAD_PAD, lanes), 1) // head_width
    for c in range(chunks):
        def spread(q):
            hit = pick_row == (q * HEAD_PAD + c * chunk_heads) + pick_head
            return jnp.where(hit, 1.0, 0.0).astype(BF16)

        grown = dot2l(table, spread(0))
        ec[c] = grown
        ed[c] = dot2l(table, spread(1))
        gain_row[c] = dot2l((table[0][0:16], table[1][0:16]), spread(2))[0:8]
        dy = dy_ref[:, c * lanes : (c + 1) * lanes]
        dyc[c] = dy
        high, low = split(grown * dy.astype(F32))
        ys_h[c] = high
        ys_l[c] = low

    own_bc.wait()
    for d in range(1, peers):
        source = lax.rem(me + d, peers)
        bc_copy(source, source).wait_recv()
    proj_b = bcr[:, 0].reshape(tokens, -1)
    proj_c = bcr[:, 1].reshape(tokens, -1)
    bcm[0] = proj_b
    bcm[1] = proj_c
    b_t = proj_b.astype(F32).T.astype(BF16)
    c_t = proj_c.astype(F32).T.astype(BF16)
    scores_t = jnp.where(upto, dot(proj_b, proj_c, NT), 0.0)
    sm[0], sm[1] = split(scores_t)
    sm[2], sm[3] = split(scores_t.T)
    for c in range(chunks):
        pulled[c] = dot2(c_t, (ys_h[c], ys_l[c]))

    @pl.when(jnp.logical_not(has_prev))
    def _():
        state_in[...] = jnp.zeros_like(state_in)

    @pl.when(jnp.logical_not(has_next))
    def _():
        pull_in[...] = jnp.zeros_like(pull_in)

    mt_acc[...] = jnp.zeros_like(mt_acc)
    bc_acc[...] = jnp.zeros_like(bc_acc)
    dcum_acc[...] = jnp.zeros_like(dcum_acc)
    dir_acc[...] = jnp.zeros_like(dir_acc)

    own_x.wait()
    for d in range(1, peers):
        source = lax.rem(me + d, peers)
        x_copy(source, source).wait_recv()
    for c in range(chunks):
        x = xr[:, :, c * lanes : (c + 1) * lanes].reshape(tokens, lanes)
        xc[c] = x
        pair = split(ed[c] * x.astype(F32))
        xs_h[c] = pair[0]
        xs_l[c] = pair[1]
        fresh[c] = dot2(b_t, pair)

    def forward_copy(c):
        return pltpu.make_async_remote_copy(
            src_ref=state_out.at[c], dst_ref=state_in.at[c],
            send_sem=send_f.at[c], recv_sem=recv_f.at[c],
            device_id={"seq": block + 1}, device_id_type=MESH,
        )

    def backward_copy(c):
        return pltpu.make_async_remote_copy(
            src_ref=pull_out.at[c], dst_ref=pull_in.at[c],
            send_sem=send_g.at[c], recv_sem=recv_g.at[c],
            device_id={"seq": block - 1}, device_id_type=MESH,
        )

    def selector(c):
        head = lax.broadcasted_iota(jnp.int32, (HEAD_PAD, lanes), 0)
        of = lax.broadcasted_iota(jnp.int32, (HEAD_PAD, lanes), 1) // head_width
        return jnp.where(head == c * chunk_heads + of, 1.0, 0.0).astype(BF16)

    def total_decay(c):
        return ec[c, tokens - 1 : tokens, :]

    def step(s, carry):
        cf = s - SKEW * block
        cb = s - SKEW * (blocks - 1 - block)
        do_f = jnp.logical_and(cf >= 0, cf < chunks)
        do_b = jnp.logical_and(cb >= 0, cb < chunks)

        @pl.when(do_f)
        def _():
            @pl.when(has_prev)
            def _():
                forward_copy(cf).wait_recv()

            state_out[cf] = total_decay(cf) * (state_in[cf] + fresh[cf])

            @pl.when(has_next)
            def _():
                forward_copy(cf).start()

        @pl.when(do_b)
        def _():
            @pl.when(has_next)
            def _():
                backward_copy(cb).wait_recv()

            @pl.when(has_prev)
            def _():
                pull_out[cb] = total_decay(cb) * pull_in[cb] + pulled[cb]
                backward_copy(cb).start()

        @pl.when(s < chunks)
        def _():
            xs = (xs_h[s], xs_l[s])
            ys = (ys_h[s], ys_l[s])
            a2_loc[s] = dot3((sm[0], sm[1]), ys)
            z_loc[s] = dot3((sm[2], sm[3]), xs)
            mt_acc[...] += dot3(xs, ys, NT)

        @pl.when(do_f)
        def _():
            entering = split(state_in[cf])
            z = z_loc[cf] + dot2(bcm[1], entering)
            bc_acc[1] += dot3((ys_h[cf], ys_l[cf]), entering, NT)
            v = split(ec[cf] * dyc[cf].astype(F32) * z)
            dcum_acc[...] += dot2(selector(cf), v, NT)

        @pl.when(do_b)
        def _():
            leaving = split(total_decay(cb) * pull_in[cb])
            a2 = a2_loc[cb] + dot2(bcm[0], leaving)
            bc_acc[0] += dot3((xs_h[cb], xs_l[cb]), leaving, NT)
            x = xc[cb].astype(F32)
            growth = ed[cb]
            gx = growth * a2 + gain_row[cb, 0:1, :] * dyc[cb].astype(F32)
            gx_ref[:, pl.ds(pl.multiple_of(cb * lanes, 128), lanes)] = gx.astype(BF16)
            direct = x * a2
            pick = selector(cb)
            dir_acc[...] += dot2(pick, split(direct), NT)
            dcum_acc[...] -= dot2(pick, split(growth * direct), NT)

        return carry

    lax.fori_loop(0, chunks + SKEW * (blocks - 1), step, 0)

    inner = jnp.where(upto, mt_acc[...], 0.0)
    grad_b = bc_acc[0] + dot2l(split(inner), bcm[1])
    grad_c = bc_acc[1] + dot2l(split(inner.T), bcm[0])
    for j in range(peers):
        part[j, 0] = grad_b[j * rows : (j + 1) * rows]
        part[j, 1] = grad_c[j * rows : (j + 1) * rows]

    def sum_copy(peer, slot):
        return pltpu.make_async_remote_copy(
            src_ref=part.at[peer], dst_ref=rs.at[slot],
            send_sem=send_r.at[peer], recv_sem=recv_r.at[slot],
            device_id={"tp": peer}, device_id_type=MESH,
        )

    for d in range(1, peers):
        sum_copy(lax.rem(me + d, peers), me).start()

    edge = jnp.zeros((HEAD_PAD, 8), F32)
    for c in range(chunks):
        both = (pull_in[c] * state_out[c]).reshape(-1, 8, lanes).sum(axis=0)
        edge = edge + dot2(selector(c), split(both), NT)
    edge = jnp.sum(edge, axis=1, keepdims=True)
    after = exact(dcum_acc[...], jnp.where(row >= col, 1.0, 0.0).astype(F32)) + edge
    gstep = jnp.exp(-cums[...]) * dir_acc[...] - rates[...] * after
    gstep_ref[...] = gstep[0:head_count]

    total = part[me]
    for d in range(1, peers):
        source = lax.rem(me + d, peers)
        sum_copy(source, source).wait_recv()
        total = total + rs[source]
    gbc_ref[...] = total

    for d in range(1, peers):
        peer = lax.rem(me + d, peers)
        bc_copy(peer, me).wait_send()
        x_copy(peer, me).wait_send()
        sum_copy(peer, me).wait_send()

    def drain(c, carry):
        @pl.when(has_next)
        def _():
            forward_copy(c).wait_send()

        @pl.when(has_prev)
        def _():
            backward_copy(c).wait_send()

        return carry

    lax.fori_loop(0, chunks, drain, 0)


def shards(x_ckpt, bc_ckpt, step_sizes, decay_rate, skip_gain, grad_out):
    peers, blocks = lax.axis_size("tp"), lax.axis_size("seq")
    rows = x_ckpt.shape[0]
    head_count, tokens = step_sizes.shape
    width = grad_out.shape[1]
    state = bc_ckpt.shape[2]
    lanes = 128
    chunks = width // lanes
    head_width = width // head_count
    wide = lambda dtype, size: pltpu.VMEM((chunks, size, lanes), dtype)
    dma = lambda n: pltpu.SemaphoreType.DMA((n,))
    vmem = pl.BlockSpec(memory_space=pltpu.VMEM)
    smem = pl.BlockSpec(memory_space=pltpu.SMEM)
    heads = pltpu.VMEM((HEAD_PAD, tokens), F32)
    return pl.pallas_call(
        partial(kernel, peers, blocks, head_width),
        out_shape=(
            jax.ShapeDtypeStruct((tokens, width), BF16),
            jax.ShapeDtypeStruct((2, rows, state), F32),
            jax.ShapeDtypeStruct((head_count, tokens), F32),
        ),
        in_specs=[vmem, vmem, vmem, smem, smem, vmem],
        out_specs=(vmem, vmem, vmem),
        scratch_shapes=[
            pltpu.VMEM((peers, rows, width), BF16),
            pltpu.VMEM((peers, 2, rows, state), BF16),
            pltpu.VMEM((peers, 2, rows, state), F32),
            pltpu.VMEM((peers, 2, rows, state), F32),
            *[wide(F32, state)] * 6,
            *[wide(F32, tokens)] * 2,
            *[wide(BF16, tokens)] * 6,
            *[wide(F32, tokens)] * 2,
            wide(F32, 8),
            heads, heads, heads, heads,
            pltpu.VMEM((tokens, tokens), F32),
            pltpu.VMEM((2, tokens, state), F32),
            heads, heads,
            pltpu.VMEM((4, tokens, tokens), BF16),
            pltpu.VMEM((2, tokens, state), BF16),
            dma(peers), dma(peers), dma(peers), dma(peers), dma(2),
            dma(chunks), dma(chunks), dma(chunks), dma(chunks),
            dma(peers), dma(peers),
        ],
        compiler_params=pltpu.CompilerParams(collective_id=0, has_side_effects=True),
    )(x_ckpt, bc_ckpt, step_sizes, decay_rate, skip_gain, grad_out)


def solution(mesh):
    return jax.shard_map(
        shards,
        mesh=mesh,
        in_specs=(
            P(("dp", "seq", "tp"), None),
            P(None, ("dp", "seq", "tp"), None),
            P("tp", ("dp", "seq")),
            P("tp"),
            P("tp"),
            P(("dp", "seq"), "tp"),
        ),
        out_specs=(
            P(("dp", "seq"), "tp"),
            P(None, ("dp", "seq", "tp"), None),
            P("tp", ("dp", "seq")),
        ),
        check_vma=False,
    )
```

time: 179 us -> 48.2 us (0.27)
  waiting for transfers between devices: 103 us -> 0 us
  Pallas kernels: 0 us -> 44.2 us
  blocking collectives: 22.6 us -> 0 us
  other arithmetic: 17.4 us -> 0 us
  between operations: 14.6 us -> 0.65 us
  matrix products: 11.7 us -> 0 us
  starting transfers between devices: 3.58 us -> 0 us
  local copies, waits for them, and re-layouts: 5.46 us -> 3.05 us
    all_gather x2 -> x0, waiting for transfers between devices: 77.2 us -> none  [carried_in(): everything = jax.tree.map(lambda part: lax.all_gather(part, axis), array)]
    pallas_call x0 -> x1, Pallas kernels: none -> 44.2 us  [shards(): pl.pallas_call(partial(kernel, peers, blocks, head_width), out_shape=(jax...]
    reduce_scatter x1 -> x0, waiting for transfers between devices: 20.5 us -> none  [shards(): lax.psum_scatter(partial_grads, 'tp', scatter_dimension=1, tiled=True)]
    unnamed x1 -> x0, blocking collectives: 12.7 us -> none
    dot_general x11 -> x0, matrix products: 11.7 us -> none  [the longest x2 3.77 us: block_step(): jnp.einsum('hts,shp->thp', weights, values, precision=highest, preferred_...]
    all_gather x1 -> x0, blocking collectives: 9.88 us -> none  [shards(): pairs = lax.all_gather(bc_ckpt, 'tp', axis=1, tiled=True)]
    select_n x8 -> x0, other arithmetic: 9.87 us -> none  [hop(): return jax.tree.map(lambda a, b: jnp.where(reached, a, b), new, before)]
    all_to_all x1 -> x0, waiting for transfers between devices: 5.35 us -> none  [shards(): lax.all_to_all(x_ckpt, 'tp', split_axis=1, concat_axis=0, tiled=True)]
  transfers between devices with their start and end apart: 4 -> 0, of which waited for: 4 -> 0; matrix products, arithmetic and copies ran while one was open for 7% -> 0% of each run, Pallas kernels for 0% -> 0%
where the time goes in v1:
time: 48.2 us; the launch traced here: 47.9 us
  Pallas kernels  44.2 us (92%)
  local copies, waits for them, and re-layouts  3.05 us (6%)
  between operations  0.65 us (1%)
    pallas_call x1, Pallas kernels, shards(): pl.pallas_call(partial(kernel, peers, blocks, head_width), out_shape=(jax...  44.2 us
    unnamed x7, local copies, waits for them, and re-layouts  3.05 us

profile of v1, /device:TPU:0, one launch (start us, length us, event | category | flops | bytes accessed | tf_op | source)
XLA Modules:
  0.0 47.9 jit_solution(5221499860853451942)
XLA Ops:
  0.6 44.2 %shard_map.85 = (bf16[128,1280]{1,0:T(8,128)(2,1)}, f32[2,32,128]{2,1,0:T(8,128)}, f32[20,128]{1,0:T(8,128)}) custom-call(bf16[32,5120]{1,0:T(8,128)(2,1)} %x_ref.1, bf16[2,32,128]{2,1,0:T(8,128)(2,1)} %bc_ref.1, f32[20,128]{1,0:T(8,128)} %step_ref.1, f32[20]{0:T(128)} %rate_ref.1, f32[20]{0:T(128)} %gain_ref.1, bf16[128,1280]{1,0:T(8,128)(2,1)} %dy_ref.1), custom_call_target="tpu_custom_call" | custom-call | tf_op jit(solution)/shard_map/pallas_call | solution.py:338
  44.9 0.0 copy-start
  44.9 1.7 %copy.12 = bf16[128,1280]{1,0:T(8,128)(2,1)} copy(bf16[128,1280]{1,0:T(8,128)(2,1)} %get-tuple-element.6) | data formatting | bytes 655360
  46.6 0.0 copy-done
  46.6 0.0 copy-start.1
  46.6 0.6 %copy.13 = f32[2,32,128]{2,1,0:T(8,128)} copy(f32[2,32,128]{2,1,0:T(8,128)S(1)} %copy-done) | data formatting | bytes 65536
  47.2 0.1 copy-done.1
  47.3 0.6 %copy.14 = f32[20,128]{1,0:T(8,128)} copy(f32[20,128]{1,0:T(8,128)S(1)} %copy-done.1) | data formatting | bytes 20480
Async XLA Ops:
  44.9 1.7 %copy-start = (f32[2,32,128]{2,1,0:T(8,128)S(1)}, f32[2,32,128]{2,1,0:T(8,128)}, u32[]{:S(2)}) copy-start(f32[2,32,128]{2,1,0:T(8,128)} %get-tuple-element.7) | copy-start | bytes 98308
  46.6 0.7 %copy-start.1 = (f32[20,128]{1,0:T(8,128)S(1)}, f32[20,128]{1,0:T(8,128)}, u32[]{:S(2)}) copy-start(f32[20,128]{1,0:T(8,128)} %get-tuple-element.8) | copy-start | bytes 30724

commit v2 on v1

--- a/solution.py
+++ b/solution.py
@@ -32,16 +32,20 @@
     return high, (v - high.astype(F32)).astype(BF16)
 
 
+def joined(a, b, dims=NN):
+    return dot(jnp.concatenate(a, axis=1), jnp.concatenate(b, axis=dims[0][1][0]), dims)
+
+
 def dot2(a, b, dims=NN):
-    return dot(a, b[0], dims) + dot(a, b[1], dims)
+    return joined((a, a), b, dims)
 
 
 def dot2l(a, b, dims=NN):
-    return dot(a[0], b, dims) + dot(a[1], b, dims)
+    return joined(a, (b, b), dims)
 
 
 def dot3(a, b, dims=NN):
-    return dot(a[0], b[0], dims) + (dot(a[0], b[1], dims) + dot(a[1], b[0], dims))
+    return joined((a[0], a[0], a[1]), (b[0], b[1], b[0]), dims)
 
 
 def kernel(
@@ -49,7 +53,7 @@
     x_ref, bc_ref, step_ref, rate_ref, gain_ref, dy_ref,
     gx_ref, gbc_ref, gstep_ref,
     xr, bcr, part, rs,
-    state_in, state_out, pull_in, pull_out, fresh, pulled, a2_loc, z_loc,
+    state_in, state_out, pull_in, pull_out, fresh, pulled,
     xs_h, xs_l, ys_h, ys_l, xc, dyc, ec, ed, gain_row,
     stp, rates, gains, cums, mt_acc, bc_acc, dcum_acc, dir_acc, sm, bcm,
     send_x, recv_x, send_b, recv_b, own_sem,
@@ -238,14 +242,15 @@
         def _():
             xs = (xs_h[s], xs_l[s])
             ys = (ys_h[s], ys_l[s])
-            a2_loc[s] = dot3((sm[0], sm[1]), ys)
-            z_loc[s] = dot3((sm[2], sm[3]), xs)
             mt_acc[...] += dot3(xs, ys, NT)
 
         @pl.when(do_f)
         def _():
             entering = split(state_in[cf])
-            z = z_loc[cf] + dot2(bcm[1], entering)
+            z = joined(
+                (sm[2], sm[2], sm[3], bcm[1], bcm[1]),
+                (xs_h[cf], xs_l[cf], xs_h[cf], *entering),
+            )
             bc_acc[1] += dot3((ys_h[cf], ys_l[cf]), entering, NT)
             v = split(ec[cf] * dyc[cf].astype(F32) * z)
             dcum_acc[...] += dot2(selector(cf), v, NT)
@@ -253,7 +258,10 @@
         @pl.when(do_b)
         def _():
             leaving = split(total_decay(cb) * pull_in[cb])
-            a2 = a2_loc[cb] + dot2(bcm[0], leaving)
+            a2 = joined(
+                (sm[0], sm[0], sm[1], bcm[0], bcm[0]),
+                (ys_h[cb], ys_l[cb], ys_h[cb], *leaving),
+            )
             bc_acc[0] += dot3((xs_h[cb], xs_l[cb]), leaving, NT)
             x = xc[cb].astype(F32)
             growth = ed[cb]
@@ -350,7 +358,6 @@
             pltpu.VMEM((peers, 2, rows, state), F32),
             pltpu.VMEM((peers, 2, rows, state), F32),
             *[wide(F32, state)] * 6,
-            *[wide(F32, tokens)] * 2,
             *[wide(BF16, tokens)] * 6,
             *[wide(F32, tokens)] * 2,
             wide(F32, 8),

time: 48.2 us -> 48 us (level)
  no operation moved by 1% of the time
where the time goes in v2:
time: 48 us; the launch traced here: 47.7 us
  Pallas kernels  44 us (92%)
  local copies, waits for them, and re-layouts  3.05 us (6%)
  between operations  0.65 us (1%)
    pallas_call x1, Pallas kernels, shards(): pl.pallas_call(partial(kernel, peers, blocks, head_width), out_shape=(jax...  44 us
    unnamed x7, local copies, waits for them, and re-layouts  3.05 us

profile of v2, /device:TPU:0, one launch (start us, length us, event | category | flops | bytes accessed | tf_op | source)
XLA Modules:
  0.0 47.7 jit_solution(10540520121103460243)
XLA Ops:
  0.6 44.0 %shard_map.85 = (bf16[128,1280]{1,0:T(8,128)(2,1)}, f32[2,32,128]{2,1,0:T(8,128)}, f32[20,128]{1,0:T(8,128)}) custom-call(bf16[32,5120]{1,0:T(8,128)(2,1)} %x_ref.1, bf16[2,32,128]{2,1,0:T(8,128)(2,1)} %bc_ref.1, f32[20,128]{1,0:T(8,128)} %step_ref.1, f32[20]{0:T(128)} %rate_ref.1, f32[20]{0:T(128)} %gain_ref.1, bf16[128,1280]{1,0:T(8,128)(2,1)} %dy_ref.1), custom_call_target="tpu_custom_call" | custom-call | tf_op jit(solution)/shard_map/pallas_call | solution.py:346
  44.7 0.0 copy-start
  44.7 1.7 %copy.12 = bf16[128,1280]{1,0:T(8,128)(2,1)} copy(bf16[128,1280]{1,0:T(8,128)(2,1)} %get-tuple-element.6) | data formatting | bytes 655360
  46.4 0.0 copy-done
  46.4 0.0 copy-start.1
  46.4 0.6 %copy.13 = f32[2,32,128]{2,1,0:T(8,128)} copy(f32[2,32,128]{2,1,0:T(8,128)S(1)} %copy-done) | data formatting | bytes 65536
  47.0 0.1 copy-done.1
  47.1 0.6 %copy.14 = f32[20,128]{1,0:T(8,128)} copy(f32[20,128]{1,0:T(8,128)S(1)} %copy-done.1) | data formatting | bytes 20480
Async XLA Ops:
  44.7 1.7 %copy-start = (f32[2,32,128]{2,1,0:T(8,128)S(1)}, f32[2,32,128]{2,1,0:T(8,128)}, u32[]{:S(2)}) copy-start(f32[2,32,128]{2,1,0:T(8,128)} %get-tuple-element.7) | copy-start | bytes 98308
  46.4 0.7 %copy-start.1 = (f32[20,128]{1,0:T(8,128)S(1)}, f32[20,128]{1,0:T(8,128)}, u32[]{:S(2)}) copy-start(f32[20,128]{1,0:T(8,128)} %get-tuple-element.8) | copy-start | bytes 30724

commit v3 on v2

--- a/solution.py
+++ b/solution.py
@@ -11,7 +11,7 @@
 F32 = jnp.float32
 BF16 = jnp.bfloat16
 HEAD_PAD = 32
-SKEW = 2
+SKEW = 3
 
 NN = (((1,), (0,)), ((), ()))
 NT = (((1,), (1,)), ((), ()))

time: 48 us -> 44.1 us (0.919)
  Pallas kernels: 44 us -> 40.2 us
    pallas_call x1, Pallas kernels: 44 us -> 40.2 us  [shards(): pl.pallas_call(partial(kernel, peers, blocks, head_width), out_shape=(jax...]
where the time goes in v3:
time: 44.1 us; the launch traced here: 43.9 us
  Pallas kernels  40.2 us (91%)
  local copies, waits for them, and re-layouts  3.05 us (7%)
  between operations  0.65 us (1%)
    pallas_call x1, Pallas kernels, shards(): pl.pallas_call(partial(kernel, peers, blocks, head_width), out_shape=(jax...  40.2 us
    unnamed x7, local copies, waits for them, and re-layouts  3.05 us

profile of v3, /device:TPU:0, one launch (start us, length us, event | category | flops | bytes accessed | tf_op | source)
XLA Modules:
  0.0 43.9 jit_solution(12511298124191454889)
XLA Ops:
  0.6 40.2 %shard_map.85 = (bf16[128,1280]{1,0:T(8,128)(2,1)}, f32[2,32,128]{2,1,0:T(8,128)}, f32[20,128]{1,0:T(8,128)}) custom-call(bf16[32,5120]{1,0:T(8,128)(2,1)} %x_ref.1, bf16[2,32,128]{2,1,0:T(8,128)(2,1)} %bc_ref.1, f32[20,128]{1,0:T(8,128)} %step_ref.1, f32[20]{0:T(128)} %rate_ref.1, f32[20]{0:T(128)} %gain_ref.1, bf16[128,1280]{1,0:T(8,128)(2,1)} %dy_ref.1), custom_call_target="tpu_custom_call" | custom-call | tf_op jit(solution)/shard_map/pallas_call | solution.py:346
  40.8 0.0 copy-start
  40.8 1.7 %copy.12 = bf16[128,1280]{1,0:T(8,128)(2,1)} copy(bf16[128,1280]{1,0:T(8,128)(2,1)} %get-tuple-element.6) | data formatting | bytes 655360
  42.6 0.0 copy-done
  42.6 0.0 copy-start.1
  42.6 0.6 %copy.13 = f32[2,32,128]{2,1,0:T(8,128)} copy(f32[2,32,128]{2,1,0:T(8,128)S(1)} %copy-done) | data formatting | bytes 65536
  43.2 0.1 copy-done.1
  43.3 0.6 %copy.14 = f32[20,128]{1,0:T(8,128)} copy(f32[20,128]{1,0:T(8,128)S(1)} %copy-done.1) | data formatting | bytes 20480
Async XLA Ops:
  40.8 1.7 %copy-start = (f32[2,32,128]{2,1,0:T(8,128)S(1)}, f32[2,32,128]{2,1,0:T(8,128)}, u32[]{:S(2)}) copy-start(f32[2,32,128]{2,1,0:T(8,128)} %get-tuple-element.7) | copy-start | bytes 98308
  42.6 0.7 %copy-start.1 = (f32[20,128]{1,0:T(8,128)S(1)}, f32[20,128]{1,0:T(8,128)}, u32[]{:S(2)}) copy-start(f32[20,128]{1,0:T(8,128)} %get-tuple-element.8) | copy-start | bytes 30724
